TPU v7x, 16 devices: a 4x2x1 block of a 4x4x8 slice. The times are simulated.
16 devices in a mesh: dp: 2 (over y, z), sp: 8 (over x, core).
Axes of the slice: x: 4, y: 2, z: 1, core: 2. Of those that a mesh axis runs over, the one named last changes fastest.
The devices are a block of a 4x4x8 slice.
Arguments:
- x: bfloat16 [8192, 3072], P(('dp', 'sp')), parts along dimension 0
- grad_out: bfloat16 [8192, 3072], P(('dp', 'sp')), parts along dimension 0
- positions: int32 [8192], P(('dp', 'sp')), parts along dimension 0
- gain: bfloat16 [3072], replicated
- w_q: bfloat16 [3072, 3072], replicated
- w_k: bfloat16 [3072, 1024], replicated
- w_v: bfloat16 [3072, 1024], replicated
- w_o: bfloat16 [3072, 3072], replicated
Outputs:
- output 1: bfloat16 [8192, 3072], P(('dp', 'sp')), parts along dimension 0
- output 2: bfloat16 [8192, 3072], P(('dp', 'sp')), parts along dimension 0
- output 3: float32 [6144, 3072], P('dp'), parts along dimension 0
- output 4: float32 [6144, 1024], P('dp'), parts along dimension 0
- output 5: float32 [6144, 1024], P('dp'), parts along dimension 0
- output 6: float32 [6144, 3072], P('dp'), parts along dimension 0
- output 7: float32 [6144], P('dp'), parts along dimension 0
There are 2 independent parts. A program takes and returns all parts, laid end to end along the dimension named above; an argument that names none is the same for every part.
All inputs are finite; a program needn't handle non-finite values.
Results may differ from a plain program's by a relative error of at most 0.0183642.
Values are sent between devices in bfloat16 or wider.
A program may use at most 768 MiB of HBM per device.

v0:
```python
import jax
import jax.numpy as jnp
from jax import lax
from jax.sharding import PartitionSpec as P

HEAD_DIM = 128
ROPE_THETA = 1000000.0
NORM_EPS = 1e-05
NEG_LARGE = -1e30
CONTRACT_ROWS = (((0,), (0,)), ((), ()))
CONTRACT_COLS = (((1,), (1,)), ((), ()))


def block_rows(seq_len, row_cost):
    row_count = seq_len
    while row_count > 8 and row_count * row_cost > 2 ** 24:
        row_count = row_count // 2
    return row_count


def rope_tables(positions):
    inv_freq = ROPE_THETA ** (-jnp.arange(0, HEAD_DIM, 2).astype(jnp.float32) / HEAD_DIM)
    angles = positions.astype(jnp.float32)[:, None] * inv_freq[None, :]
    return jnp.cos(angles)[:, None, :], jnp.sin(angles)[:, None, :]


def rotate(values, cos_t, sin_t):
    half_dim = values.shape[-1] // 2
    lower_half = values[..., :half_dim]
    upper_half = values[..., half_dim:]
    return jnp.concatenate([lower_half * cos_t - upper_half * sin_t, upper_half * cos_t + lower_half * sin_t], axis=-1)


def attn_forward(q_all, k_all, v_all):
    seq_len, kv_loc, group_size, head_dim = q_all.shape
    row_count = block_rows(seq_len, kv_loc * group_size * seq_len)
    n_blocks = seq_len // row_count
    qk_scale = head_dim ** -0.5
    key_index = jnp.arange(seq_len)
    q_blocks = q_all.reshape(n_blocks, row_count, kv_loc, group_size, head_dim)
    blk_starts = jnp.arange(n_blocks) * row_count

    def one_block(block_args):
        q_blk, blk_start = block_args
        scores = jnp.einsum('qhgd,khd->hgqk', q_blk, k_all, preferred_element_type=jnp.float32) * qk_scale
        causal = (blk_start + jnp.arange(row_count))[:, None] >= key_index[None, :]
        attn_prob = jax.nn.softmax(jnp.where(causal, scores, NEG_LARGE), axis=-1)
        blk_out = jnp.einsum('hgqk,khd->qhgd', attn_prob.astype(jnp.bfloat16), v_all, preferred_element_type=jnp.float32)
        return blk_out.astype(jnp.bfloat16)

    return lax.map(one_block, (q_blocks, blk_starts)).reshape(seq_len, kv_loc, group_size, head_dim)


def attn_backward(q_all, k_all, v_all, do_all):
    seq_len, kv_loc, group_size, head_dim = q_all.shape
    row_count = block_rows(seq_len, kv_loc * group_size * seq_len)
    n_blocks = seq_len // row_count
    qk_scale = head_dim ** -0.5
    key_index = jnp.arange(seq_len)
    q_blocks = q_all.reshape(n_blocks, row_count, kv_loc, group_size, head_dim)
    do_blocks = do_all.reshape(n_blocks, row_count, kv_loc, group_size, head_dim)
    blk_starts = jnp.arange(n_blocks) * row_count

    def one_block(acc_pair, block_args):
        dk_acc, dv_acc = acc_pair
        q_blk, do_blk, blk_start = block_args
        scores = jnp.einsum('qhgd,khd->hgqk', q_blk, k_all, preferred_element_type=jnp.float32) * qk_scale
        causal = (blk_start + jnp.arange(row_count))[:, None] >= key_index[None, :]
        attn_prob = jax.nn.softmax(jnp.where(causal, scores, NEG_LARGE), axis=-1)
        prob_bf = attn_prob.astype(jnp.bfloat16)
        dv_acc = dv_acc + jnp.einsum('hgqk,qhgd->khd', prob_bf, do_blk, preferred_element_type=jnp.float32)
        d_prob = jnp.einsum('qhgd,khd->hgqk', do_blk, v_all, preferred_element_type=jnp.float32)
        d_score = attn_prob * (d_prob - jnp.sum(attn_prob * d_prob, axis=-1, keepdims=True)) * qk_scale
        ds_bf = d_score.astype(jnp.bfloat16)
        dq_blk = jnp.einsum('hgqk,khd->qhgd', ds_bf, k_all, preferred_element_type=jnp.float32)
        dk_acc = dk_acc + jnp.einsum('hgqk,qhgd->khd', ds_bf, q_blk, preferred_element_type=jnp.float32)
        return (dk_acc, dv_acc), dq_blk.astype(jnp.bfloat16)

    zero_acc = jnp.zeros((seq_len, kv_loc, head_dim), jnp.float32)
    (dk_all, dv_all), dq_blocks = lax.scan(one_block, (zero_acc, zero_acc), (q_blocks, do_blocks, blk_starts))
    return dq_blocks.reshape(seq_len, kv_loc, group_size, head_dim), dk_all, dv_all


def solution(mesh):
    sp_size = mesh.shape['sp']
    seq_spec = P(('dp', 'sp'), None)
    pos_spec = P(('dp', 'sp'))
    replicated = P(None, None)
    part_rows = P('dp', None)

    def local_step(x, grad_out, positions, gain, w_q, w_k, w_v, w_o):
        tok_count = x.shape[0]
        n_heads = w_q.shape[1] // HEAD_DIM
        kv_heads = w_k.shape[1] // HEAD_DIM
        kv_copies = max(1, sp_size // kv_heads)
        q_loc = n_heads // sp_size
        kv_loc = max(kv_heads, sp_size) // sp_size
        group_size = q_loc // kv_loc
        seq_len = tok_count * sp_size
        x_f = x.astype(jnp.float32)
        inv_rms = lax.rsqrt(jnp.mean(x_f * x_f, axis=-1, keepdims=True) + NORM_EPS)
        normed = x_f * inv_rms
        gain_f = gain.astype(jnp.float32)
        hidden = (normed * gain_f).astype(jnp.bfloat16)
        cos_t, sin_t = rope_tables(positions)
        q_proj = jnp.dot(hidden, w_q, preferred_element_type=jnp.float32).reshape(tok_count, n_heads, HEAD_DIM)
        k_proj = jnp.dot(hidden, w_k, preferred_element_type=jnp.float32).reshape(tok_count, kv_heads, HEAD_DIM)
        v_send = jnp.dot(hidden, w_v, preferred_element_type=jnp.float32).astype(jnp.bfloat16).reshape(tok_count, kv_heads, HEAD_DIM)
        q_rot = rotate(q_proj, cos_t, sin_t).astype(jnp.bfloat16)
        k_send = rotate(k_proj, cos_t, sin_t).astype(jnp.bfloat16)
        if kv_copies > 1:
            k_send = jnp.repeat(k_send, kv_copies, axis=1)
            v_send = jnp.repeat(v_send, kv_copies, axis=1)
        q_all = lax.all_to_all(q_rot, 'sp', 1, 0, tiled=True).reshape(seq_len, kv_loc, group_size, HEAD_DIM)
        k_all = lax.all_to_all(k_send, 'sp', 1, 0, tiled=True)
        v_all = lax.all_to_all(v_send, 'sp', 1, 0, tiled=True)
        o_all = attn_forward(q_all, k_all, v_all)
        o_loc = lax.all_to_all(o_all.reshape(seq_len, q_loc, HEAD_DIM), 'sp', 0, 1, tiled=True).reshape(tok_count, n_heads * HEAD_DIM)
        mixed = jnp.dot(o_loc, w_o, preferred_element_type=jnp.float32)
        result = (x_f + mixed).astype(jnp.bfloat16)
        grad_wo = lax.psum(lax.dot_general(o_loc, grad_out, CONTRACT_ROWS, preferred_element_type=jnp.float32), 'sp')
        d_o = lax.dot_general(grad_out, w_o, CONTRACT_COLS, preferred_element_type=jnp.float32).astype(jnp.bfloat16)
        do_all = lax.all_to_all(d_o.reshape(tok_count, n_heads, HEAD_DIM), 'sp', 1, 0, tiled=True).reshape(seq_len, kv_loc, group_size, HEAD_DIM)
        dq_all, dk_all, dv_all = attn_backward(q_all, k_all, v_all, do_all)
        dq_loc = lax.all_to_all(dq_all.reshape(seq_len, q_loc, HEAD_DIM), 'sp', 0, 1, tiled=True)
        dk_loc = lax.all_to_all(dk_all.astype(jnp.bfloat16), 'sp', 0, 1, tiled=True)
        dv_loc = lax.all_to_all(dv_all.astype(jnp.bfloat16), 'sp', 0, 1, tiled=True)
        dk_sum = jnp.sum(dk_loc.reshape(tok_count, kv_heads, kv_copies, HEAD_DIM), axis=2, dtype=jnp.float32)
        dv_sum = jnp.sum(dv_loc.reshape(tok_count, kv_heads, kv_copies, HEAD_DIM), axis=2, dtype=jnp.float32)
        dq_pre = rotate(dq_loc.astype(jnp.float32), cos_t, -sin_t).astype(jnp.bfloat16).reshape(tok_count, n_heads * HEAD_DIM)
        dk_pre = rotate(dk_sum, cos_t, -sin_t).astype(jnp.bfloat16).reshape(tok_count, kv_heads * HEAD_DIM)
        dv_pre = dv_sum.astype(jnp.bfloat16).reshape(tok_count, kv_heads * HEAD_DIM)
        grad_wq = lax.psum(lax.dot_general(hidden, dq_pre, CONTRACT_ROWS, preferred_element_type=jnp.float32), 'sp')
        grad_wk = lax.psum(lax.dot_general(hidden, dk_pre, CONTRACT_ROWS, preferred_element_type=jnp.float32), 'sp')
        grad_wv = lax.psum(lax.dot_general(hidden, dv_pre, CONTRACT_ROWS, preferred_element_type=jnp.float32), 'sp')
        d_hidden = (lax.dot_general(dq_pre, w_q, CONTRACT_COLS, preferred_element_type=jnp.float32)
                    + lax.dot_general(dk_pre, w_k, CONTRACT_COLS, preferred_element_type=jnp.float32)
                    + lax.dot_general(dv_pre, w_v, CONTRACT_COLS, preferred_element_type=jnp.float32))
        grad_gain = lax.psum(jnp.sum(d_hidden * normed, axis=0), 'sp')
        d_normed = d_hidden * gain_f
        d_xnorm = inv_rms * (d_normed - normed * jnp.mean(d_normed * normed, axis=-1, keepdims=True))
        grad_x = (grad_out.astype(jnp.float32) + d_xnorm).astype(jnp.bfloat16)
        return result, grad_x, grad_wq, grad_wk, grad_wv, grad_wo, grad_gain

    return jax.shard_map(local_step, mesh=mesh,
                         in_specs=(seq_spec, seq_spec, pos_spec, P(None), replicated, replicated, replicated, replicated),
                         out_specs=(seq_spec, seq_spec, part_rows, part_rows, part_rows, part_rows, P('dp')),
                         check_vma=False)
```

profile of v0, /device:TPU:112, one launch (start us, length us, event | category | flops | bytes accessed | tf_op | source)
XLA Modules:
  0.0 2408.4 jit_solution(8439574535808672227)
XLA Ops:
  98.5 28.1 %all-to-all-done = bf16[512,24,128]{2,0,1:T(8,128)(2,1)S(1)} async-done(((bf16[512,24,128]{2,0,1:T(8,128)(2,1)}), bf16[512,24,128]{2,0,1:T(8,128)(2,1)S(1)}, u32[]{:S(2)}, u32[]{:S(2)}) %all-to-all-start) | async-done | bytes 3145760 | tf_op jit(solution)/shard_map/all_to_all | solution.py:114
  148.9 713.6 %while.27 = (s32[]{:T(128)}, f32[4096,1,128]{0,2,1:T(8,128)}, f32[4096,1,128]{0,2,1:T(8,128)}, bf16[4,1024,1,3,128]{4,1,0,3,2:T(8,128)(2,1)}, bf16[4,1024,1,3,12...) while((s32[]{:T(128)}, f32[4096,1,128]{0,2,1:T(8,128)}, ...), condition=%wide.region_9.10_spmd.clone, body=%wide.region_5.9_spmd.clone.sunk | while | flops 16439959552 | bytes 502149344 | solution.py:80
  177.3 23.5 fusion.145
  200.8 24.0 fusion.149
  224.8 36.7 %fusion.146 = (f32[3,1024]{1,0:T(4,128)S(1)}, f32[1024,3,4096]{2,0,1:T(8,128)}) fusion(f32[3,1024]{1,0:T(4,128)S(1)} %fusion.145, f32[3,1024]{1,0:T(4,128)S(1)} %get-tuple-element.382, f32[1024,3,4096]{2,0,1:T(8,128)} %get-tuple-element.381, pred[1024,4096]{1,0:T(8,128)(4,1)} %copy-done, bf16[4096,1,128]{2,0,1:T(8,128)(2,1)} %get-tuple-element.436, ...), kind=kOutput, calls=%fused_computation.25.clone.1 | convolution fusion | flops 3296719872 | bytes 106729472 | tf_op jit(solution)/shard_map/while/body/eval_jaxpr/qhgd,khd->hgqk/dot_general | solution.py:72
  261.5 41.7 %fusion.147 = bf16[3,1024,4096]{2,1,0:T(8,128)(2,1)} fusion(f32[1024,3,4096]{2,0,1:T(8,128)} %get-tuple-element.383, f32[3,1024]{1,0:T(4,128)S(1)} %get-tuple-element.384, f32[3,1024]{1,0:T(4,128)S(1)} %fusion.145, f32[3,1024]{1,0:T(4,128)S(1)} %get-tuple-element.382, f32[1024,3,4096]{2,0,1:T(8,128)} %get-tuple-element.381, pred[1024,4096]{1,0:T(8,128)(4,1)} %copy-done), kind=kLoop, calls=%fused_computation.33.clone.1 | loop fusion | flops 100663296 | bytes 130060288 | tf_op jit(solution)/shard_map/reshape.35
  355.1 23.5 fusion.145
  378.6 24.6 %fusion.149 = f32[4096,1,128]{0,2,1:T(8,128)} fusion(f32[3,1024]{1,0:T(4,128)S(1)} %fusion.145, f32[3,1024]{1,0:T(4,128)S(1)} %get-tuple-element.382, f32[1024,3,4096]{2,0,1:T(8,128)} %get-tuple-element.381, pred[1024,4096]{1,0:T(8,128)(4,1)} %copy-done, f32[4096,1,128]{0,2,1:T(8,128)} %get-tuple-element.419, pred[]{:T(512)S(6)} %compare.3, ...), kind=kOutput, calls=%fused_computation.40.clone.1 | convolution fusion | flops 3285188608 | bytes 59531268 | tf_op jit(solution)/shard_map/while/body/eval_jaxpr/hgqk,qhgd->khd/dot_general | solution.py:71
  403.3 36.6 %fusion.146 = (f32[3,1024]{1,0:T(4,128)S(1)}, f32[1024,3,4096]{2,0,1:T(8,128)}) fusion(f32[3,1024]{1,0:T(4,128)S(1)} %fusion.145, f32[3,1024]{1,0:T(4,128)S(1)} %get-tuple-element.382, f32[1024,3,4096]{2,0,1:T(8,128)} %get-tuple-element.381, pred[1024,4096]{1,0:T(8,128)(4,1)} %copy-done, bf16[4096,1,128]{2,0,1:T(8,128)(2,1)} %get-tuple-element.436, ...), kind=kOutput, calls=%fused_computation.25.clone.1 | convolution fusion | flops 3296719872 | bytes 106729472 | tf_op jit(solution)/shard_map/while/body/eval_jaxpr/qhgd,khd->hgqk/dot_general | solution.py:72
  439.9 41.7 %fusion.147 = bf16[3,1024,4096]{2,1,0:T(8,128)(2,1)} fusion(f32[1024,3,4096]{2,0,1:T(8,128)} %get-tuple-element.383, f32[3,1024]{1,0:T(4,128)S(1)} %get-tuple-element.384, f32[3,1024]{1,0:T(4,128)S(1)} %fusion.145, f32[3,1024]{1,0:T(4,128)S(1)} %get-tuple-element.382, f32[1024,3,4096]{2,0,1:T(8,128)} %get-tuple-element.381, pred[1024,4096]{1,0:T(8,128)(4,1)} %copy-done), kind=kLoop, calls=%fused_computation.33.clone.1 | loop fusion | flops 100663296 | bytes 130060288 | tf_op jit(solution)/shard_map/reshape.35
  533.5 23.5 fusion.145
  557.0 24.6 %fusion.149 = f32[4096,1,128]{0,2,1:T(8,128)} fusion(f32[3,1024]{1,0:T(4,128)S(1)} %fusion.145, f32[3,1024]{1,0:T(4,128)S(1)} %get-tuple-element.382, f32[1024,3,4096]{2,0,1:T(8,128)} %get-tuple-element.381, pred[1024,4096]{1,0:T(8,128)(4,1)} %copy-done, f32[4096,1,128]{0,2,1:T(8,128)} %get-tuple-element.419, pred[]{:T(512)S(6)} %compare.3, ...), kind=kOutput, calls=%fused_computation.40.clone.1 | convolution fusion | flops 3285188608 | bytes 59531268 | tf_op jit(solution)/shard_map/while/body/eval_jaxpr/hgqk,qhgd->khd/dot_general | solution.py:71
  581.7 36.7 %fusion.146 = (f32[3,1024]{1,0:T(4,128)S(1)}, f32[1024,3,4096]{2,0,1:T(8,128)}) fusion(f32[3,1024]{1,0:T(4,128)S(1)} %fusion.145, f32[3,1024]{1,0:T(4,128)S(1)} %get-tuple-element.382, f32[1024,3,4096]{2,0,1:T(8,128)} %get-tuple-element.381, pred[1024,4096]{1,0:T(8,128)(4,1)} %copy-done, bf16[4096,1,128]{2,0,1:T(8,128)(2,1)} %get-tuple-element.436, ...), kind=kOutput, calls=%fused_computation.25.clone.1 | convolution fusion | flops 3296719872 | bytes 106729472 | tf_op jit(solution)/shard_map/while/body/eval_jaxpr/qhgd,khd->hgqk/dot_general | solution.py:72
  618.3 41.7 %fusion.147 = bf16[3,1024,4096]{2,1,0:T(8,128)(2,1)} fusion(f32[1024,3,4096]{2,0,1:T(8,128)} %get-tuple-element.383, f32[3,1024]{1,0:T(4,128)S(1)} %get-tuple-element.384, f32[3,1024]{1,0:T(4,128)S(1)} %fusion.145, f32[3,1024]{1,0:T(4,128)S(1)} %get-tuple-element.382, f32[1024,3,4096]{2,0,1:T(8,128)} %get-tuple-element.381, pred[1024,4096]{1,0:T(8,128)(4,1)} %copy-done), kind=kLoop, calls=%fused_computation.33.clone.1 | loop fusion | flops 100663296 | bytes 130060288 | tf_op jit(solution)/shard_map/reshape.35
  735.5 24.6 %fusion.149 = f32[4096,1,128]{0,2,1:T(8,128)} fusion(f32[3,1024]{1,0:T(4,128)S(1)} %fusion.145, f32[3,1024]{1,0:T(4,128)S(1)} %get-tuple-element.382, f32[1024,3,4096]{2,0,1:T(8,128)} %get-tuple-element.381, pred[1024,4096]{1,0:T(8,128)(4,1)} %copy-done, f32[4096,1,128]{0,2,1:T(8,128)} %get-tuple-element.419, pred[]{:T(512)S(6)} %compare.3, ...), kind=kOutput, calls=%fused_computation.40.clone.1 | convolution fusion | flops 3285188608 | bytes 59531268 | tf_op jit(solution)/shard_map/while/body/eval_jaxpr/hgqk,qhgd->khd/dot_general | solution.py:71
  760.1 36.6 %fusion.146 = (f32[3,1024]{1,0:T(4,128)S(1)}, f32[1024,3,4096]{2,0,1:T(8,128)}) fusion(f32[3,1024]{1,0:T(4,128)S(1)} %fusion.145, f32[3,1024]{1,0:T(4,128)S(1)} %get-tuple-element.382, f32[1024,3,4096]{2,0,1:T(8,128)} %get-tuple-element.381, pred[1024,4096]{1,0:T(8,128)(4,1)} %copy-done, bf16[4096,1,128]{2,0,1:T(8,128)(2,1)} %get-tuple-element.436, ...), kind=kOutput, calls=%fused_computation.25.clone.1 | convolution fusion | flops 3296719872 | bytes 106729472 | tf_op jit(solution)/shard_map/while/body/eval_jaxpr/qhgd,khd->hgqk/dot_general | solution.py:72
  796.7 41.7 %fusion.147 = bf16[3,1024,4096]{2,1,0:T(8,128)(2,1)} fusion(f32[1024,3,4096]{2,0,1:T(8,128)} %get-tuple-element.383, f32[3,1024]{1,0:T(4,128)S(1)} %get-tuple-element.384, f32[3,1024]{1,0:T(4,128)S(1)} %fusion.145, f32[3,1024]{1,0:T(4,128)S(1)} %get-tuple-element.382, f32[1024,3,4096]{2,0,1:T(8,128)} %get-tuple-element.381, pred[1024,4096]{1,0:T(8,128)(4,1)} %copy-done), kind=kLoop, calls=%fused_computation.33.clone.1 | loop fusion | flops 100663296 | bytes 130060288 | tf_op jit(solution)/shard_map/reshape.35
  893.4 299.6 %while.26 = (s32[]{:T(128)}, bf16[4,1024,1,3,128]{4,1,0,3,2:T(8,128)(2,1)S(1)}, s32[4]{0:T(128)}, bf16[4,1024,1,3,128]{4,1,3,2,0:T(8,128)(2,1)}, bf16[4096,1,128...) while((s32[]{:T(128)}, bf16[4,1024,1,3,128]{4,1,0,3,2:T(8,128)(2,1)S(1)}, ...), condition=%wide.region_4.5_spmd.clone, body=%wide.region_1.4_spmd.clone.sunk | while | flops 6598028288 | bytes 188297360 | solution.py:51
  921.8 23.5 fusion.136
  1226.8 29.0 %all-to-all-done.3 = bf16[4096,3,128]{2,1,0:T(4,128)(2,1)} async-done(((bf16[4096,3,128]{2,1,0:T(4,128)(2,1)}), bf16[4096,3,128]{2,1,0:T(4,128)(2,1)}, u32[]{:S(2)}, u32[]{:S(2)}) %all-to-all-start.3) | async-done | bytes 3145760 | tf_op jit(solution)/shard_map/all_to_all | solution.py:118
  1394.7 24.3 %psum.39 = f32[3072]{0:T(1024)} all-reduce(f32[3072]{0:T(1024)S(1)} %get-tuple-element.223), channel_id=1, replica_groups=mesh['dp'=2,'sp'=8] {'sp'}, use_global_device_ids=true, to_apply=%region_16.17 | all-reduce | flops 3072 | bytes 24576 | tf_op jit(solution)/shard_map/psum | solution.py:139
  1440.5 880.8 %all-reduce.3.cloned.1.call-done = (f32[3072,3072]{1,0:T(8,128)}, f32[3072,1024]{1,0:T(8,128)}, f32[3072,1024]{1,0:T(8,128)}, f32[3072,3072]{1,0:T(8,128)}) async-done(((f32[3072,3072]{1,0:T(8,128)}, f32[3072,1024]{1,0:T(8,128)}, f32[3072,1024]{1,0:T(8,128)}, f32[3072,3072]{1,0:T(8,128)}), (f32[3072,3072]{1,0:T(8,128)}, f32[3072,1024]{1,0:T(8,128)}, f32[3072,1024]{1,0:T(8,128)}, ...) | async-done | bytes 100663312 | tf_op jit(solution)/shard_map/psum | solution.py:133
  2321.3 27.9 %copy.191 = f32[3072,3072]{1,0:T(8,128)} copy(f32[3072,3072]{1,0:T(8,128)} %get-tuple-element.441) | data formatting | bytes 75497472
  2373.4 27.9 %copy.194 = f32[3072,3072]{1,0:T(8,128)} copy(f32[3072,3072]{1,0:T(8,128)} %get-tuple-element.444) | data formatting | bytes 75497472
  (214 shorter events, 868.5 us)
Async XLA Ops:
  9.8 78.6 %copy-start.26 = (f32[512]{0:T(512)}, f32[512]{0:T(512)S(1)}, u32[]{:S(2)}) copy-start(f32[512]{0:T(512)S(1)} %add_rsqrt_fusion) | copy-start | bytes 6148
  10.5 77.9 %copy-start.24 = (f32[3072]{0:T(1024)}, f32[3072]{0:T(1024)S(1)}, u32[]{:S(2)}) copy-start(f32[3072]{0:T(1024)S(1)} %convert_element_type.123) | copy-start | bytes 36868
  19.0 21.7 all-to-all-start.2
  40.7 43.4 %all-to-all-start.4 = ((bf16[512,24,128]{2,0,1:T(8,128)(2,1)}), bf16[512,24,128]{2,0,1:T(8,128)(2,1)}, u32[]{:S(2)}, u32[]{:S(2)}) async-start(bf16[512,24,128]{2,0,1:T(8,128)(2,1)} %bitcast.239), calls=%async_computation.4 | async-start | bytes 6291456 | tf_op jit(solution)/shard_map/all_to_all | solution.py:123
  62.3 33.9 %copy-start.9 = (f32[512,64]{1,0:T(8,128)}, f32[512,64]{1,0:T(8,128)S(1)}, u32[]{:S(2)}) copy-start(f32[512,64]{1,0:T(8,128)S(1)} %get-tuple-element.279) | copy-start | bytes 393220
  84.1 42.5 %all-to-all-start = ((bf16[512,24,128]{2,0,1:T(8,128)(2,1)}), bf16[512,24,128]{2,0,1:T(8,128)(2,1)S(1)}, u32[]{:S(2)}, u32[]{:S(2)}) async-start(bf16[512,24,128]{2,0,1:T(8,128)(2,1)} %pad_maximum_fusion), calls=%async_computation | async-start | bytes 6291456 | tf_op jit(solution)/shard_map/all_to_all | solution.py:114
  126.6 20.2 all-to-all-start.1
  154.0 23.3 copy-start
  261.5 41.7 %copy-start.2 = (f32[4096,1,128]{0,2,1:T(8,128)S(1)}, f32[4096,1,128]{0,2,1:T(8,128)}, u32[]{:S(2)}) copy-start(f32[4096,1,128]{0,2,1:T(8,128)} %get-tuple-element.418) | copy-start | bytes 6291460 | tf_op jit(solution)/shard_map/while
  331.8 23.3 copy-start
  439.9 41.7 %copy-start.2 = (f32[4096,1,128]{0,2,1:T(8,128)S(1)}, f32[4096,1,128]{0,2,1:T(8,128)}, u32[]{:S(2)}) copy-start(f32[4096,1,128]{0,2,1:T(8,128)} %get-tuple-element.418) | copy-start | bytes 6291460 | tf_op jit(solution)/shard_map/while
  510.2 23.3 copy-start
  618.3 41.7 %copy-start.2 = (f32[4096,1,128]{0,2,1:T(8,128)S(1)}, f32[4096,1,128]{0,2,1:T(8,128)}, u32[]{:S(2)}) copy-start(f32[4096,1,128]{0,2,1:T(8,128)} %get-tuple-element.418) | copy-start | bytes 6291460 | tf_op jit(solution)/shard_map/while
  688.7 23.3 copy-start
  796.7 41.7 %copy-start.2 = (f32[4096,1,128]{0,2,1:T(8,128)S(1)}, f32[4096,1,128]{0,2,1:T(8,128)}, u32[]{:S(2)}) copy-start(f32[4096,1,128]{0,2,1:T(8,128)} %get-tuple-element.418) | copy-start | bytes 6291460 | tf_op jit(solution)/shard_map/while
  868.0 19.5 all-to-all-start.6
  888.4 313.1 %all-to-all-start.7 = ((bf16[8,2,32768]{2,1,0:T(2,128)(2,1)}), bf16[8,2,32768]{2,1,0:T(2,128)(2,1)}, u32[]{:S(2)}, u32[]{:S(2)}) async-start(bf16[8,2,32768]{2,1,0:T(2,128)(2,1)} %reshape.260), calls=%async_computation.7 | async-start | bytes 2097152 | tf_op jit(solution)/shard_map/all_to_all | solution.py:127
  973.3 23.3 copy-start.1
  1048.0 23.3 copy-start.1
  1122.8 23.3 copy-start.1
  1201.6 54.2 %all-to-all-start.3 = ((bf16[4096,3,128]{2,1,0:T(4,128)(2,1)}), bf16[4096,3,128]{2,1,0:T(4,128)(2,1)}, u32[]{:S(2)}, u32[]{:S(2)}) async-start(bf16[4096,3,128]{2,1,0:T(4,128)(2,1)} %copy.119), calls=%async_computation.3 | async-start | bytes 8388608 | tf_op jit(solution)/shard_map/all_to_all | solution.py:118
  1226.8 33.8 %copy-start.12 = (bf16[8,2,32768]{2,1,0:T(2,128)(2,1)S(1)}, bf16[8,2,32768]{2,1,0:T(2,128)(2,1)}, u32[]{:S(2)}) copy-start(bf16[8,2,32768]{2,1,0:T(2,128)(2,1)} %copy-done.11) | copy-start | bytes 3145732
  1255.8 54.2 %all-to-all-start.5 = ((bf16[4096,3,128]{2,1,0:T(4,128)(2,1)}), bf16[4096,3,128]{2,1,0:T(4,128)(2,1)}, u32[]{:S(2)}, u32[]{:S(2)}) async-start(bf16[4096,3,128]{2,1,0:T(4,128)(2,1)} %copy.127), calls=%async_computation.5 | async-start | bytes 8388608 | tf_op jit(solution)/shard_map/all_to_all | solution.py:125
  1260.5 1060.7 %all-reduce.3.cloned.1.call-start = ((), (), s32[]{:S(2)}) async-start(), calls=%async_computation.8 | async-start | bytes 201326592 | tf_op jit(solution)/shard_map/psum | solution.py:133
  (26 other events, 257.4 us)
Sparse Core Ops, SparseCore 0:
  1358.8 962.3 all-reduce.2
where the time goes:
time: 2420 us; the launch traced here: 2410 us
  waiting for transfers between devices  973 us (40%)
  matrix products  760 us (31%)
  other arithmetic  423 us (17%)
  local copies, waits for them, and re-layouts  174 us (7%)
  starting transfers between devices  36.9 us (2%)
  blocking collectives  24.3 us (1%)
    psum x1, waiting for transfers between devices, local_step(): lax.psum(lax.dot_general(hidden, dq_pre, CONTRACT_ROWS, preferred_element...  881 us
    reduce_sum x8, other arithmetic, one_block(): attn_prob = jax.nn.softmax(jnp.where(causal, scores, NEG_LARGE), axis=-1)  188 us
    dot_general x8, matrix products, one_block(): jnp.einsum('qhgd,khd->hgqk', q_blk, k_all, preferred_element_type=jnp.flo...  186 us
    another operation x8, other arithmetic  179 us
    dot_general x4, matrix products, one_block(): jnp.einsum('qhgd,khd->hgqk', do_blk, v_all, preferred_element_type=jnp.fl...  147 us
    unnamed x64, local copies, waits for them, and re-layouts  102 us
    dot_general x4, matrix products, one_block(): jnp.einsum('hgqk,qhgd->khd', prob_bf, do_blk, preferred_element_type=jnp....  97.9 us
    dot_general x4, matrix products, one_block(): jnp.einsum('hgqk,khd->qhgd', attn_prob.astype(jnp.bfloat16), v_all, prefe...  92 us
  transfers between devices with their start and end apart: 9, of which 7 were waited for; matrix products, arithmetic and copies ran while one was open for 20% of the time, Pallas kernels for 0%

commit v1 on v0

v1 whole, which is shorter than its diff:
```python
import functools

import jax
import jax.numpy as jnp
from jax import lax
from jax.experimental import pallas as pl
from jax.experimental.pallas import tpu as pltpu
from jax.sharding import PartitionSpec as P

HEAD = 128
HALF = HEAD // 2
ROPE_THETA = 1000000.0
NORM_EPS = 1e-05
NEG_LARGE = -1e30
LOG2E = 1.4426950408889634
QK_SCALE = HEAD ** -0.5
EXP_SCALE = QK_SCALE * LOG2E
BLK = 512
F32 = jnp.float32
BF16 = jnp.bfloat16
VMEM_MAX = 60 * 2 ** 20
NN = (((1,), (0,)), ((), ()))
NT = (((1,), (1,)), ((), ()))
TN = (((0,), (0,)), ((), ()))


def dot(a, b, dims=NN):
    return lax.dot_general(a, b, dims, preferred_element_type=F32)


def params(limit=VMEM_MAX):
    return pltpu.CompilerParams(vmem_limit_bytes=limit)


def cost(flops, nbytes):
    return pl.CostEstimate(flops=int(flops), bytes_accessed=int(nbytes), transcendentals=0)


def qkv_kernel(q_heads, wT_ref, hT_ref, cos_ref, sin_ref, q_ref, qT_ref, k_ref, kT_ref, vT_ref):
    projT = dot(wT_ref[...], hT_ref[0])
    cos_t = cos_ref[...]
    sin_t = sin_ref[...]

    def rope(block):
        low, high = block[:HALF], block[HALF:]
        return jnp.concatenate([low * cos_t - high * sin_t, high * cos_t + low * sin_t], axis=0)

    for head in range(q_heads):
        rot = rope(projT[head * HEAD:(head + 1) * HEAD])
        qT_ref[head] = rot.astype(BF16)
        q_ref[head] = rot.T.astype(BF16)
    base = q_heads * HEAD
    rot = rope(projT[base:base + HEAD])
    kT_ref[...] = rot.astype(BF16)
    k_ref[...] = rot.T.astype(BF16)
    vT_ref[...] = projT[base + HEAD:base + 2 * HEAD].astype(BF16)


def qkv_call(wT, hT_all, cosT, sinT, q_heads):
    shards, d_model, tok = hT_all.shape
    seq = shards * tok
    rows = wT.shape[0]
    return pl.pallas_call(
        functools.partial(qkv_kernel, q_heads),
        grid=(shards,),
        in_specs=[pl.BlockSpec((rows, d_model), lambda j: (0, 0)),
                  pl.BlockSpec((1, d_model, tok), lambda j: (j, 0, 0)),
                  pl.BlockSpec((HALF, tok), lambda j: (0, j)),
                  pl.BlockSpec((HALF, tok), lambda j: (0, j))],
        out_specs=[pl.BlockSpec((q_heads, tok, HEAD), lambda j: (0, j, 0)),
                   pl.BlockSpec((q_heads, HEAD, tok), lambda j: (0, 0, j)),
                   pl.BlockSpec((tok, HEAD), lambda j: (j, 0)),
                   pl.BlockSpec((HEAD, tok), lambda j: (0, j)),
                   pl.BlockSpec((HEAD, tok), lambda j: (0, j))],
        out_shape=[jax.ShapeDtypeStruct((q_heads, seq, HEAD), BF16),
                   jax.ShapeDtypeStruct((q_heads, HEAD, seq), BF16),
                   jax.ShapeDtypeStruct((seq, HEAD), BF16),
                   jax.ShapeDtypeStruct((HEAD, seq), BF16),
                   jax.ShapeDtypeStruct((HEAD, seq), BF16)],
        compiler_params=params(),
        cost_estimate=cost(2 * rows * d_model * seq, 2 * d_model * seq),
        name='qkv',
    )(wT, hT_all, cosT, sinT)


def fwd_kernel(q_heads, qT_ref, k_ref, vT_ref, oT_ref, lse_ref, m_ref, l_ref, acc_ref):
    i = pl.program_id(0)
    m_ref[...] = jnp.full(m_ref.shape, NEG_LARGE, F32)
    l_ref[...] = jnp.zeros(l_ref.shape, F32)
    acc_ref[...] = jnp.zeros(acc_ref.shape, F32)

    def step(j, masked):
        rows = pl.ds(pl.multiple_of(j * BLK, BLK), BLK)
        k_blk = k_ref[rows, :]
        vT_blk = vT_ref[:, rows]
        for head in range(q_heads):
            s = dot(k_blk, qT_ref[head])
            if masked:
                key = lax.broadcasted_iota(jnp.int32, s.shape, 0)
                qry = lax.broadcasted_iota(jnp.int32, s.shape, 1)
                s = jnp.where(key <= qry, s, NEG_LARGE)
            m_old = m_ref[head]
            m_new = jnp.maximum(m_old, jnp.max(s, axis=0, keepdims=True))
            m_ref[head] = m_new
            p = jnp.exp2(s * EXP_SCALE - m_new * EXP_SCALE)
            alpha = jnp.exp2((m_old - m_new) * EXP_SCALE)
            l_ref[head] = l_ref[head] * alpha + jnp.sum(p, axis=0, keepdims=True)
            acc_ref[head] = acc_ref[head] * alpha + dot(vT_blk, p.astype(BF16))

    lax.fori_loop(0, i, lambda j, _: (step(j, False), 0)[1], 0)
    step(i, True)
    for head in range(q_heads):
        l = l_ref[head]
        oT_ref[head] = (acc_ref[head] / l).astype(BF16)
        lse = m_ref[head] * EXP_SCALE + jnp.log2(l)
        lse_ref[head] = jnp.broadcast_to(lse, (HEAD, BLK)).T


def fwd_call(qT, k, vT):
    q_heads, _, seq = qT.shape
    n_blk = seq // BLK
    return pl.pallas_call(
        functools.partial(fwd_kernel, q_heads),
        grid=(n_blk,),
        in_specs=[pl.BlockSpec((q_heads, HEAD, BLK), lambda i: (0, 0, i)),
                  pl.BlockSpec((seq, HEAD), lambda i: (0, 0)),
                  pl.BlockSpec((HEAD, seq), lambda i: (0, 0))],
        out_specs=[pl.BlockSpec((q_heads, HEAD, BLK), lambda i: (0, 0, i)),
                   pl.BlockSpec((q_heads, BLK, HEAD), lambda i: (0, i, 0))],
        out_shape=[jax.ShapeDtypeStruct((q_heads, HEAD, seq), BF16),
                   jax.ShapeDtypeStruct((q_heads, seq, HEAD), F32)],
        scratch_shapes=[pltpu.VMEM((q_heads, 1, BLK), F32),
                        pltpu.VMEM((q_heads, 1, BLK), F32),
                        pltpu.VMEM((q_heads, HEAD, BLK), F32)],
        compiler_params=params(),
        cost_estimate=cost(4 * q_heads * HEAD * seq * seq, 4 * q_heads * HEAD * seq),
        name='attn_fwd',
    )(qT, k, vT)


def do_kernel(q_heads, dy_ref, woT_ref, oT_ref, do_ref, doT_ref, delta_ref):
    d_o = dot(dy_ref[...], woT_ref[...])
    for head in range(q_heads):
        blk = d_o[:, head * HEAD:(head + 1) * HEAD].astype(BF16)
        blkT = blk.astype(F32).T
        do_ref[head] = blk
        doT_ref[head] = blkT.astype(BF16)
        delta = jnp.sum(blkT * oT_ref[head].astype(F32), axis=0, keepdims=True)
        delta_ref[head] = jnp.broadcast_to(delta, (HEAD, delta.shape[1])).T


def do_call(dy_all, woT, oT):
    seq, d_model = dy_all.shape
    q_heads = oT.shape[0]
    return pl.pallas_call(
        functools.partial(do_kernel, q_heads),
        grid=(seq // BLK,),
        in_specs=[pl.BlockSpec((BLK, d_model), lambda i: (i, 0)),
                  pl.BlockSpec((d_model, q_heads * HEAD), lambda i: (0, 0)),
                  pl.BlockSpec((q_heads, HEAD, BLK), lambda i: (0, 0, i))],
        out_specs=[pl.BlockSpec((q_heads, BLK, HEAD), lambda i: (0, i, 0)),
                   pl.BlockSpec((q_heads, HEAD, BLK), lambda i: (0, 0, i)),
                   pl.BlockSpec((q_heads, BLK, HEAD), lambda i: (0, i, 0))],
        out_shape=[jax.ShapeDtypeStruct((q_heads, seq, HEAD), BF16),
                   jax.ShapeDtypeStruct((q_heads, HEAD, seq), BF16),
                   jax.ShapeDtypeStruct((q_heads, seq, HEAD), F32)],
        compiler_params=params(),
        cost_estimate=cost(2 * seq * d_model * q_heads * HEAD, 2 * seq * d_model),
        name='d_o',
    )(dy_all, woT, oT)


def bwd_kernel(first, last, n_blk, *refs):
    (q_ref, qT_ref, do_ref, doT_ref, lse_ref, delta_ref, k_ref, kT_ref, vT_ref,
     cos_ref, sin_ref, cosT_ref, sinT_ref) = refs[:13]
    refs = refs[13:]
    if not first:
        dk_in, dv_in = refs[:2]
        refs = refs[2:]
    dq_ref, dk_out, dv_out, dq_acc, dk_acc, dv_acc = refs
    j = pl.program_id(0)

    @pl.when(j == 0)
    def _():
        dq_acc[...] = jnp.zeros(dq_acc.shape, F32)

    if first:
        dk_acc[...] = jnp.zeros(dk_acc.shape, F32)
        dv_acc[...] = jnp.zeros(dv_acc.shape, F32)
    else:
        dk_acc[...] = dk_in[...]
        dv_acc[...] = dv_in[...]
    k_blk = k_ref[...]
    kT_blk = kT_ref[...]
    vT_blk = vT_ref[...]

    def step(i, masked):
        rows = pl.ds(pl.multiple_of(i * BLK, BLK), BLK)
        s = dot(q_ref[0, rows, :], kT_blk)
        dp = dot(do_ref[0, rows, :], vT_blk)
        lse = lse_ref[0, rows, :]
        delta = delta_ref[0, rows, :]
        reps = BLK // HEAD
        p = jnp.exp2(s * EXP_SCALE - jnp.concatenate([lse] * reps, axis=1))
        if masked:
            qry = lax.broadcasted_iota(jnp.int32, s.shape, 0)
            key = lax.broadcasted_iota(jnp.int32, s.shape, 1)
            p = jnp.where(key <= qry, p, 0.0)
        ds = p * (dp - jnp.concatenate([delta] * reps, axis=1))
        p_bf = p.astype(BF16)
        ds_bf = ds.astype(BF16)
        dv_acc[...] += dot(doT_ref[0, :, rows], p_bf)
        dk_acc[...] += dot(qT_ref[0, :, rows], ds_bf)
        dq_acc[rows, :] += dot(ds_bf, k_blk)

    step(j, True)
    lax.fori_loop(j + 1, n_blk, lambda i, _: (step(i, False), 0)[1], 0)
    rows = pl.ds(pl.multiple_of(j * BLK, BLK), BLK)
    dq = dq_acc[rows, :] * QK_SCALE
    dq_ref[...] = (dq * cos_ref[...] + pltpu.roll(dq, HALF, 1) * sin_ref[...]).astype(BF16)
    if last:
        dk = dk_acc[...] * QK_SCALE
        low, high = dk[:HALF], dk[HALF:]
        cos_t, sin_t = cosT_ref[...], sinT_ref[...]
        pre = jnp.concatenate([low * cos_t + high * sin_t, high * cos_t - low * sin_t], axis=0)
        dk_out[...] = pre.T.astype(BF16)
        dv_out[...] = dv_acc[...].T.astype(BF16)
    else:
        dk_out[...] = dk_acc[...]
        dv_out[...] = dv_acc[...]


def bwd_call(head, n_heads, ops, dkv):
    q, qT, d_o, doT, lse, delta, k, kT, vT, cos, sin, cosT, sinT = ops
    seq = k.shape[0]
    n_blk = seq // BLK
    first, last = head == 0, head == n_heads - 1
    row_all = pl.BlockSpec((1, seq, HEAD), lambda j: (head, 0, 0))
    colT_all = pl.BlockSpec((1, HEAD, seq), lambda j: (head, 0, 0))
    row_blk = pl.BlockSpec((BLK, HEAD), lambda j: (j, 0))
    colT_blk = pl.BlockSpec((HEAD, BLK), lambda j: (0, j))
    half_blk = pl.BlockSpec((HALF, BLK), lambda j: (0, j))
    in_specs = [row_all, colT_all, row_all, colT_all, row_all, row_all,
                row_blk, colT_blk, colT_blk, row_blk, row_blk, half_blk, half_blk]
    args = list(ops)
    if not first:
        in_specs += [colT_blk, colT_blk]
        args += list(dkv)
    if last:
        kv_spec, kv_shape = row_blk, jax.ShapeDtypeStruct((seq, HEAD), BF16)
    else:
        kv_spec, kv_shape = colT_blk, jax.ShapeDtypeStruct((HEAD, seq), F32)
    dq, dk, dv = pl.pallas_call(
        functools.partial(bwd_kernel, first, last, n_blk),
        grid=(n_blk,),
        in_specs=in_specs,
        out_specs=[row_blk, kv_spec, kv_spec],
        out_shape=[jax.ShapeDtypeStruct((seq, HEAD), BF16), kv_shape, kv_shape],
        scratch_shapes=[pltpu.VMEM((seq, HEAD), F32), pltpu.VMEM((HEAD, BLK), F32), pltpu.VMEM((HEAD, BLK), F32)],
        compiler_params=params(),
        cost_estimate=cost(10 * HEAD * seq * seq, 12 * HEAD * seq),
        name='attn_bwd',
    )(*args)
    return dq, (dk, dv)


def dw_kernel(shards, tok, row_blk, stride, offset, aliased, *refs):
    hT_any, d_any = refs[:2]
    out_any, lhs, rhs, acc, lhs_sem, rhs_sem, out_sem = refs[2 + aliased:]
    d_model = hT_any.shape[1]
    steps = d_model // row_blk

    def lhs_copy(step, slot, j):
        return pltpu.make_async_copy(hT_any.at[j, pl.ds(step * row_blk, row_blk), :],
                                     lhs.at[slot, :, pl.ds(j * tok, tok)], lhs_sem.at[slot, j])

    def rhs_copy(j):
        return pltpu.make_async_copy(d_any.at[j], rhs.at[:, pl.ds(j * HEAD, HEAD)], rhs_sem.at[j])

    def out_copy(step, slot, j):
        return pltpu.make_async_copy(
            acc.at[slot, :, pl.ds(j * HEAD, HEAD)],
            out_any.at[pl.ds(step * row_blk, row_blk), pl.ds((j * stride + offset) * HEAD, HEAD)],
            out_sem.at[slot, j])

    for j in range(shards):
        lhs_copy(0, 0, j).start()
    for j in range(shards):
        rhs_copy(j).start()
    for step in range(steps):
        slot = step % 2
        if step + 1 < steps:
            for j in range(shards):
                lhs_copy(step + 1, 1 - slot, j).start()
        for j in range(shards):
            lhs_copy(step, slot, j).wait()
        if step >= 2:
            for j in range(shards):
                out_copy(step - 2, slot, j).wait()
        for pair in range(shards // 2):
            if step == 0:
                rhs_copy(2 * pair).wait()
                rhs_copy(2 * pair + 1).wait()
            cols = pl.ds(pair * 2 * HEAD, 2 * HEAD)
            acc[slot, :, cols] = dot(lhs[slot], rhs[:, cols])
            out_copy(step, slot, 2 * pair).start()
            out_copy(step, slot, 2 * pair + 1).start()
    for step in range(max(0, steps - 2), steps):
        for j in range(shards):
            out_copy(step, step % 2, j).wait()


def dw_call(hT_all, d_all, stride, offset, width, prev):
    shards, d_model, tok = hT_all.shape
    seq = shards * tok
    row_blk = 512
    aliased = 0 if prev is None else 1
    args = [hT_all, d_all] + ([] if prev is None else [prev])
    return pl.pallas_call(
        functools.partial(dw_kernel, shards, tok, row_blk, stride, offset, aliased),
        in_specs=[pl.BlockSpec(memory_space=pl.ANY)] * len(args),
        out_specs=pl.BlockSpec(memory_space=pl.ANY),
        out_shape=jax.ShapeDtypeStruct((d_model, width), F32),
        scratch_shapes=[pltpu.VMEM((2, row_blk, seq), BF16),
                        pltpu.VMEM((seq, shards * HEAD), BF16),
                        pltpu.VMEM((2, row_blk, shards * HEAD), F32),
                        pltpu.SemaphoreType.DMA((2, shards)),
                        pltpu.SemaphoreType.DMA((shards,)),
                        pltpu.SemaphoreType.DMA((2, shards))],
        input_output_aliases={} if prev is None else {2: 0},
        compiler_params=params(),
        cost_estimate=cost(2 * seq * d_model * shards * HEAD, 2 * seq * (d_model + shards * HEAD)),
        name='d_w',
    )(*args)


def solution(mesh):
    sp_size = mesh.shape['sp']
    seq_spec = P(('dp', 'sp'), None)
    replicated = P(None, None)
    part_rows = P('dp', None)

    def local_step(x, grad_out, positions, gain, w_q, w_k, w_v, w_o):
        tok, d_model = x.shape
        n_heads = w_q.shape[1] // HEAD
        q_loc = n_heads // sp_size
        seq = tok * sp_size
        me = lax.axis_index('sp')
        x_f = x.astype(F32)
        inv_rms = lax.rsqrt(jnp.mean(x_f * x_f, axis=-1, keepdims=True) + NORM_EPS)
        normed = x_f * inv_rms
        gain_f = gain.astype(F32)
        hidden = (normed * gain_f).astype(BF16)
        hT_all = lax.all_gather(hidden.T, 'sp', axis=0)
        pos_all = lax.all_gather(positions, 'sp', axis=0, tiled=True)
        dy_src, _ = lax.optimization_barrier((grad_out, hidden))
        dy_all = lax.all_gather(dy_src, 'sp', axis=0, tiled=True)

        inv_freq = ROPE_THETA ** (-jnp.arange(0, HEAD, 2).astype(F32) / HEAD)
        anglesT = inv_freq[:, None] * pos_all.astype(F32)[None, :]
        cosT, sinT = jnp.cos(anglesT), jnp.sin(anglesT)
        cos = jnp.concatenate([cosT, cosT], axis=0).T
        sin = jnp.concatenate([sinT, -sinT], axis=0).T

        q_cols = q_loc * HEAD
        wq_own = lax.dynamic_slice_in_dim(w_q, me * q_cols, q_cols, 1)
        wk_own = lax.dynamic_slice_in_dim(w_k, me * HEAD, HEAD, 1)
        wv_own = lax.dynamic_slice_in_dim(w_v, me * HEAD, HEAD, 1)
        wT = jnp.concatenate([wq_own, wk_own, wv_own], axis=1).T
        woT = lax.dynamic_slice_in_dim(w_o, me * q_cols, q_cols, 0).T

        q, qT, k, kT, vT = qkv_call(wT, hT_all, cosT, sinT, q_loc)
        oT, lse = fwd_call(qT, k, vT)
        oT_all = lax.all_gather(oT, 'sp', axis=0).reshape(n_heads * HEAD, seq)
        d_o, doT, delta = do_call(dy_all, woT, oT)
        ops = (q, qT, d_o, doT, lse, delta, k, kT, vT, cos, sin, cosT, sinT)
        dkv = None
        dq_alls = []
        for head in range(q_loc):
            dq, dkv = bwd_call(head, q_loc, ops, dkv)
            dq_alls.append(lax.all_gather(dq, 'sp', axis=0))
        dk_all = lax.all_gather(dkv[0], 'sp', axis=0)
        dv_all = lax.all_gather(dkv[1], 'sp', axis=0)

        oT_loc = lax.dynamic_slice_in_dim(oT_all, me * tok, tok, 1)
        mixed = dot(oT_loc, w_o, TN)
        result = (x_f + mixed).astype(BF16)
        grad_wo = dot(oT_all, dy_all)

        grad_wq = None
        for head in range(q_loc):
            grad_wq = dw_call(hT_all, dq_alls[head], q_loc, head, n_heads * HEAD, grad_wq)
        grad_wk = dw_call(hT_all, dk_all, 1, 0, sp_size * HEAD, None)
        grad_wv = dw_call(hT_all, dv_all, 1, 0, sp_size * HEAD, None)

        def own(d_all):
            return lax.dynamic_slice_in_dim(d_all, me * tok, tok, 1)

        dq_own = jnp.stack([own(d) for d in dq_alls], axis=1)
        dq_own = dq_own.transpose(2, 0, 1, 3).reshape(tok, n_heads * HEAD)
        dk_own = own(dk_all).transpose(1, 0, 2).reshape(tok, sp_size * HEAD)
        dv_own = own(dv_all).transpose(1, 0, 2).reshape(tok, sp_size * HEAD)
        d_hidden = dot(dq_own, w_q, NT) + dot(dk_own, w_k, NT) + dot(dv_own, w_v, NT)
        grad_gain = lax.psum(jnp.sum(d_hidden * normed, axis=0), 'sp')
        d_normed = d_hidden * gain_f
        d_xnorm = inv_rms * (d_normed - normed * jnp.mean(d_normed * normed, axis=-1, keepdims=True))
        grad_x = (grad_out.astype(F32) + d_xnorm).astype(BF16)
        return result, grad_x, grad_wq, grad_wk, grad_wv, grad_wo, grad_gain

    return jax.shard_map(local_step, mesh=mesh,
                         in_specs=(seq_spec, seq_spec, P(('dp', 'sp')), P(None),
                                   replicated, replicated, replicated, replicated),
                         out_specs=(seq_spec, seq_spec, part_rows, part_rows, part_rows, part_rows, P('dp')),
                         check_vma=False)
```

time: 2420 us -> 985 us (0.41)
  waiting for transfers between devices: 973 us -> 287 us
  matrix products: 760 us -> 138 us
  Pallas kernels: 0 us -> 396 us
  other arithmetic: 423 us -> 27 us
  local copies, waits for them, and re-layouts: 174 us -> 66.1 us
  starting transfers between devices: 36.9 us -> 0.5 us
  blocking collectives: 24.3 us -> 51 us
    psum x1 -> x0, waiting for transfers between devices: 881 us -> none  [local_step(): lax.psum(lax.dot_general(hidden, dq_pre, CONTRACT_ROWS, preferred_element...]
    dot_general x40 -> x5, matrix products: 760 us -> 138 us  [dot(): return lax.dot_general(a, b, dims, preferred_element_type=F32)]
    pallas_call x0 -> x11, Pallas kernels: none -> 396 us  [the longest x5 184 us: dw_call(): pl.pallas_call(functools.partial(dw_kernel, shards, tok, row_blk, stride,...]
    all_gather x0 -> x8, waiting for transfers between devices: none -> 283 us  [the longest x3 133 us: local_step(): dq_alls.append(lax.all_gather(dq, 'sp', axis=0))]
    reduce_sum x9 -> x0, other arithmetic: 188 us -> none  [the longest x8 188 us: one_block(): attn_prob = jax.nn.softmax(jnp.where(causal, scores, NEG_LARGE), axis=-1)]
    another operation x8 -> x0, other arithmetic: 179 us -> none
    all_to_all x8 -> x0, waiting for transfers between devices: 92.7 us -> none  [the longest x1 29 us: local_step(): lax.all_to_all(o_all.reshape(seq_len, q_loc, HEAD_DIM), 'sp', 0, 1, tiled...]
    unnamed x64 -> x26, local copies, waits for them, and re-layouts: 102 us -> 8.96 us
  transfers between devices with their start and end apart: 9 -> 8, of which waited for: 7 -> 6; matrix products, arithmetic and copies ran while one was open for 20% -> 12% of each run, Pallas kernels for 0% -> 28%
where the time goes in v1:
time: 985 us; the launch traced here: 980 us
  Pallas kernels  396 us (40%)
  waiting for transfers between devices  287 us (29%)
  matrix products  138 us (14%)
  local copies, waits for them, and re-layouts  66.1 us (7%)
  blocking collectives  51 us (5%)
  other arithmetic  27 us (3%)
  between operations  14.6 us (1%)
    pallas_call x5, Pallas kernels, dw_call(): pl.pallas_call(functools.partial(dw_kernel, shards, tok, row_blk, stride,...  184 us
    dot_general x5, matrix products, dot(): return lax.dot_general(a, b, dims, preferred_element_type=F32)  138 us
    all_gather x3, waiting for transfers between devices, local_step(): dq_alls.append(lax.all_gather(dq, 'sp', axis=0))  133 us
    pallas_call x3, Pallas kernels, bwd_call(): pl.pallas_call(functools.partial(bwd_kernel, first, last, n_blk), grid=(n...  100 us
    all_gather x1, waiting for transfers between devices, local_step(): hT_all = lax.all_gather(hidden.T, 'sp', axis=0)  64.1 us
    pallas_call x1, Pallas kernels, fwd_call(): pl.pallas_call(functools.partial(fwd_kernel, q_heads), grid=(n_blk,), in_...  64 us
    all_gather x1, waiting for transfers between devices, local_step(): dv_all = lax.all_gather(dkv[1], 'sp', axis=0)  45.4 us
    all_gather x1, waiting for transfers between devices, local_step(): dk_all = lax.all_gather(dkv[0], 'sp', axis=0)  40.8 us
  transfers between devices with their start and end apart: 8, of which 6 were waited for; matrix products, arithmetic and copies ran while one was open for 12% of the time, Pallas kernels for 28%

profile of v1, /device:TPU:112, one launch (start us, length us, event | category | flops | bytes accessed | tf_op | source)
XLA Modules:
  0.0 980.2 jit_solution(8293758065325082254)
XLA Ops:
  25.2 24.6 %all-gather.7 = s32[8,1,512]{2,1,0:T(1,128)S(1)} all-gather(s32[1,1,512]{2,1,0:T(1,128)S(1)} %bitcast.63), channel_id=1, replica_groups=mesh['dp'=2,'sp'=8] {'sp'}, dimensions={0}, use_global_device_ids=true | all-gather | bytes 18432 | tf_op jit(solution)/shard_map/all_gather | solution.py:355
  71.7 64.1 %all-gather.19.cloned.1.call-done = bf16[24576,512]{0,1:T(8,128)(2,1)} async-done(((bf16[3072,512]{0,1:T(8,128)(2,1)}), bf16[24576,512]{0,1:T(8,128)(2,1)}) %all-gather.19.cloned.1.call-update) | async-done | bytes 25165840 | tf_op jit(solution)/shard_map/all_gather | solution.py:354
  135.8 32.6 %copy.58 = bf16[24576,512]{1,0:T(8,128)(2,1)} copy(bf16[24576,512]{0,1:T(8,128)(2,1)} %all-gather.19.cloned.1.call-done) | data formatting | bytes 50331648 | tf_op jit(solution)/shard_map/all_gather | solution.py:354
  168.4 24.2 %qkv.1 = (bf16[3,4096,128]{2,1,0:T(8,128)(2,1)}, bf16[3,128,4096]{2,1,0:T(8,128)(2,1)}, bf16[4096,128]{1,0:T(8,128)(2,1)}, bf16[128,4096]{1,0:T(8,128)(2,1)}, bf16[128,4096]{1,0:T(8,128)(2,1)}) custom-call(bf16[640,3072]{1,0:T(8,128)(2,1)} %maximum_bitcast_fusion.wT_ref, bf16[8,3072,512]{2,1,0:T(8,128)(2,1)} %bitcast.42, f32[64,4096]{1,0:T(8,128)} %copy-done.3, ...), custom_call_target="tpu_custom_call" | custom-call | flops 16106127360 | bytes 25165824 | tf_op jit(solution)/shard_map/qkv/pallas_call | solution.py:63
  192.7 64.0 %attn_fwd.1 = (bf16[3,128,4096]{2,1,0:T(8,128)(2,1)}, f32[3,4096,128]{2,1,0:T(8,128)}) custom-call(bf16[3,128,4096]{2,1,0:T(8,128)(2,1)} %get-tuple-element.27.qT_ref.refs_1_, bf16[4096,128]{1,0:T(8,128)(2,1)} %get-tuple-element.28.k_ref.refs_6_, bf16[128,4096]{1,0:T(8,128)(2,1)} %get-tuple-element.29.vT_ref.refs_8_), custom_call_target="tpu_custom_call" | custom-call | flops 25769803776 | bytes 6291456 | tf_op jit(solution)/shard_map/attn_fwd/pallas_call | solution.py:122
  256.7 23.4 %d_o.1 = (bf16[3,4096,128]{2,1,0:T(8,128)(2,1)}, bf16[3,128,4096]{2,1,0:T(8,128)(2,1)}, f32[3,4096,128]{2,1,0:T(8,128)}) custom-call(bf16[4096,3072]{1,0:T(8,128)(2,1)} %all-gather.17.cloned.1.call-done.dy_ref, bf16[3072,384]{1,0:T(8,128)(2,1)} %bitcast.53, bf16[3,128,4096]{2,1,0:T(8,128)(2,1)} %get-tuple-element.30.oT_ref), custom_call_target="tpu_custom_call" | custom-call | flops 9663676416 | bytes 25165824 | tf_op jit(solution)/shard_map/d_o/pallas_call | solution.py:155
  280.1 33.0 %attn_bwd.3 = (bf16[4096,128]{1,0:T(8,128)(2,1)}, f32[128,4096]{1,0:T(8,128)}, f32[128,4096]{1,0:T(8,128)}) custom-call(bf16[3,4096,128]{2,1,0:T(8,128)(2,1)} %get-tuple-element.31.refs_0_, bf16[3,128,4096]{2,1,0:T(8,128)(2,1)} %get-tuple-element.27.qT_ref.refs_1_, bf16[3,4096,128]{2,1,0:T(8,128)(2,1)} %get-tuple-element.33.refs_2_, ...), custom_call_target="tpu_custom_call" | custom-call | flops 21474836480 | bytes 6291456 | tf_op jit(solution)/shard_map/attn_bwd/pallas_call | solution.py:253
  313.1 33.3 %attn_bwd.4 = (bf16[4096,128]{1,0:T(8,128)(2,1)}, f32[128,4096]{1,0:T(8,128)}, f32[128,4096]{1,0:T(8,128)}) custom-call(bf16[3,4096,128]{2,1,0:T(8,128)(2,1)} %get-tuple-element.31.refs_0_, bf16[3,128,4096]{2,1,0:T(8,128)(2,1)} %get-tuple-element.27.qT_ref.refs_1_, bf16[3,4096,128]{2,1,0:T(8,128)(2,1)} %get-tuple-element.33.refs_2_, ...), custom_call_target="tpu_custom_call" | custom-call | flops 21474836480 | bytes 6291456 | tf_op jit(solution)/shard_map/attn_bwd/pallas_call | solution.py:253
  346.5 33.8 %attn_bwd.5 = (bf16[4096,128]{1,0:T(8,128)(2,1)}, bf16[4096,128]{1,0:T(8,128)(2,1)}, bf16[4096,128]{1,0:T(8,128)(2,1)}) custom-call(bf16[3,4096,128]{2,1,0:T(8,128)(2,1)} %get-tuple-element.31.refs_0_, bf16[3,128,4096]{2,1,0:T(8,128)(2,1)} %get-tuple-element.27.qT_ref.refs_1_, bf16[3,4096,128]{2,1,0:T(8,128)(2,1)} %get-tuple-element.33.refs_2_, ...), custom_call_target="tpu_custom_call" | custom-call | flops 21474836480 | bytes 6291456 | tf_op jit(solution)/shard_map/attn_bwd/pallas_call | solution.py:253
  383.9 42.9 %all-gather.27.cloned.1.call-done = bf16[32768,128]{1,0:T(8,128)(2,1)} async-done(((bf16[4096,128]{1,0:T(8,128)(2,1)}), bf16[32768,128]{1,0:T(8,128)(2,1)}) %all-gather.27.cloned.1.call-update) | async-done | bytes 8388624 | tf_op jit(solution)/shard_map/all_gather | solution.py:381
  429.1 44.9 %all-gather.25.cloned.1.call-done = bf16[32768,128]{1,0:T(8,128)(2,1)} async-done(((bf16[4096,128]{1,0:T(8,128)(2,1)}), bf16[32768,128]{1,0:T(8,128)(2,1)}) %all-gather.25.cloned.1.call-update) | async-done | bytes 8388624 | tf_op jit(solution)/shard_map/all_gather | solution.py:381
  476.2 44.9 %all-gather.23.cloned.1.call-done = bf16[32768,128]{1,0:T(8,128)(2,1)} async-done(((bf16[4096,128]{1,0:T(8,128)(2,1)}), bf16[32768,128]{1,0:T(8,128)(2,1)}) %all-gather.23.cloned.1.call-update) | async-done | bytes 8388624 | tf_op jit(solution)/shard_map/all_gather | solution.py:381
  527.4 40.8 %all-gather.29.cloned.1.call-done = bf16[32768,128]{1,0:T(8,128)(2,1)} async-done(((bf16[4096,128]{1,0:T(8,128)(2,1)}), bf16[32768,128]{1,0:T(8,128)(2,1)}) %all-gather.29.cloned.1.call-update) | async-done | bytes 8388624 | tf_op jit(solution)/shard_map/all_gather | solution.py:382
  570.0 45.4 %all-gather.31.cloned.1.call-done = bf16[32768,128]{1,0:T(8,128)(2,1)} async-done(((bf16[4096,128]{1,0:T(8,128)(2,1)}), bf16[32768,128]{1,0:T(8,128)(2,1)}) %all-gather.31.cloned.1.call-update) | async-done | bytes 8388624 | tf_op jit(solution)/shard_map/all_gather | solution.py:383
  626.5 8.4 fusion.17
  634.9 17.9 %fusion.10 = (f32[3072]{0:T(1024)S(1)}, f32[512]{0:T(512)S(1)}, f32[512,3072]{1,0:T(8,128)}) fusion(bf16[512,3072]{1,0:T(8,128)(2,1)S(1)} %copy-done, f32[512]{0:T(512)S(1)} %copy-done.9, f32[3072]{0:T(1024)S(1)} %copy-done.7, f32[512,3072]{1,0:T(8,128)} %fusion.17, f32[512,3072]{1,0:T(8,128)} %fusion.16, bf16[512,3072]{0,1:T(8,128)(2,1)S(1)} %bitcast.52, ...), kind=kOutput, calls=%fused_computation.13 | convolution fusion | flops 9677828096 | bytes 44068864 | tf_op jit(solution)/shard_map/dot_general | solution.py:28
  652.8 26.4 %psum.7 = f32[3072]{0:T(1024)} all-reduce(f32[3072]{0:T(1024)S(1)} %get-tuple-element.47), channel_id=1, replica_groups=mesh['dp'=2,'sp'=8] {'sp'}, use_global_device_ids=true, to_apply=%region_3.0 | all-reduce | flops 3072 | bytes 24576 | tf_op jit(solution)/shard_map/psum | solution.py:404
  685.5 36.7 %d_w.5.refs_2_ = f32[3072,3072]{1,0:T(8,128)} custom-call(bf16[8,3072,512]{2,1,0:T(8,128)(2,1)} %bitcast.43, bf16[8,4096,128]{2,1,0:T(8,128)(2,1)} %bitcast.57), custom_call_target="tpu_custom_call" | custom-call | flops 25769803776 | bytes 33554432 | tf_op jit(solution)/shard_map/d_w/pallas_call | solution.py:319
  722.3 36.9 %d_w.8 = f32[3072,1024]{1,0:T(8,128)} custom-call(bf16[8,3072,512]{2,1,0:T(8,128)(2,1)} %bitcast.44, bf16[8,4096,128]{2,1,0:T(8,128)(2,1)} %bitcast.59), custom_call_target="tpu_custom_call" | custom-call | flops 25769803776 | bytes 33554432 | tf_op jit(solution)/shard_map/d_w/pallas_call | solution.py:319
  759.2 36.9 %d_w.9 = f32[3072,1024]{1,0:T(8,128)} custom-call(bf16[8,3072,512]{2,1,0:T(8,128)(2,1)} %bitcast.45, bf16[8,4096,128]{2,1,0:T(8,128)(2,1)} %bitcast.61), custom_call_target="tpu_custom_call" | custom-call | flops 25769803776 | bytes 33554432 | tf_op jit(solution)/shard_map/d_w/pallas_call | solution.py:319
  796.1 36.9 %d_w.6.refs_2_ = f32[3072,3072]{1,0:T(8,128)} custom-call(bf16[8,3072,512]{2,1,0:T(8,128)(2,1)} %bitcast.46, bf16[8,4096,128]{2,1,0:T(8,128)(2,1)} %bitcast.51, f32[3072,3072]{1,0:T(8,128)} %d_w.5.refs_2_), custom_call_target="tpu_custom_call", output_to_operand_aliasing={{}: (2, {})} | custom-call | flops 25769803776 | bytes 33554432 | tf_op jit(solution)/shard_map/d_w/pallas_call | solution.py:319
  833.0 36.7 %d_w.7 = f32[3072,3072]{1,0:T(8,128)} custom-call(bf16[8,3072,512]{2,1,0:T(8,128)(2,1)} %bitcast.47, bf16[8,4096,128]{2,1,0:T(8,128)(2,1)} %bitcast.49, f32[3072,3072]{1,0:T(8,128)} %d_w.6.refs_2_), custom_call_target="tpu_custom_call", output_to_operand_aliasing={{}: (2, {})} | custom-call | flops 25769803776 | bytes 33554432 | tf_op jit(solution)/shard_map/d_w/pallas_call | solution.py:319
  869.8 16.2 %fusion.12 = bf16[512,3072]{1,0:T(8,128)(2,1)} fusion(bf16[512,3072]{1,0:T(8,128)(2,1)S(1)} %copy-done, bf16[3072,3072]{1,0:T(8,128)(2,1)} %param.15, bf16[3072,4096]{1,0:T(8,128)(2,1)} %bitcast.64, s32[]{:T(128)S(6)} %select_n.8), kind=kOutput, calls=%fused_computation.15 | convolution fusion | flops 9668395008 | bytes 28311556 | tf_op jit(solution)/shard_map/dot_general | solution.py:28
  886.0 87.1 %fusion.18 = f32[3072,3072]{1,0:T(8,128)} fusion(bf16[3072,4096]{1,0:T(8,128)(2,1)} %bitcast.65, bf16[4096,3072]{1,0:T(8,128)(2,1)} %all-gather.17.cloned.1.call-done.dy_ref), kind=kOutput, calls=%fused_computation.40 | convolution fusion | flops 77309411328 | bytes 88080384 | tf_op jit(solution)/shard_map/dot_general | solution.py:28
  (70 shorter events, 73.3 us)
Async XLA Ops:
  7.2 128.7 %all-gather.19.cloned.1.call-start = ((), (), s32[]{:S(2)}) async-start(), calls=%async_computation.1 | async-start | bytes 28311552 | tf_op jit(solution)/shard_map/all_gather | solution.py:354
  7.9 2.6 copy-start.6
  10.5 0.6 copy-start.8
  15.9 240.8 %all-gather.17.cloned.1.call-start = ((), (), s32[]{:S(2)}) async-start(), calls=%async_computation | async-start | bytes 28311552 | tf_op jit(solution)/shard_map/all_gather | solution.py:357
  16.7 410.0 %all-gather.27.cloned.1.call-start = ((), (), s32[]{:S(2)}) async-start(), calls=%async_computation.5 | async-start | bytes 9437184 | tf_op jit(solution)/shard_map/all_gather | solution.py:381
  18.7 6.4 copy-start.10
  57.8 1.0 copy-start.3
  57.8 9.3 copy-start.2
  58.7 8.3 copy-start.1
  380.3 93.6 %all-gather.25.cloned.1.call-start = ((), (), s32[]{:S(2)}) async-start(), calls=%async_computation.4 | async-start | bytes 9437184 | tf_op jit(solution)/shard_map/all_gather | solution.py:381
  381.0 140.1 %all-gather.23.cloned.1.call-start = ((), (), s32[]{:S(2)}) async-start(), calls=%async_computation.3 | async-start | bytes 9437184 | tf_op jit(solution)/shard_map/all_gather | solution.py:381
  381.6 186.6 %all-gather.29.cloned.1.call-start = ((), (), s32[]{:S(2)}) async-start(), calls=%async_computation.6 | async-start | bytes 9437184 | tf_op jit(solution)/shard_map/all_gather | solution.py:382
  382.3 233.2 %all-gather.31.cloned.1.call-start = ((), (), s32[]{:S(2)}) async-start(), calls=%async_computation.7 | async-start | bytes 9437184 | tf_op jit(solution)/shard_map/all_gather | solution.py:383
  383.1 486.7 %all-gather.21.cloned.1.call-start = ((), (), s32[]{:S(2)}) async-start(), calls=%async_computation.2 | async-start | bytes 28311552 | tf_op jit(solution)/shard_map/all_gather | solution.py:374
  618.1 8.3 copy-start.5
  626.4 8.4 copy-start
  626.4 8.4 copy-start.4
  626.4 8.4 copy-start.7
  626.5 8.4 copy-start.9
Sparse Core Ops, SparseCore 0:
  16.1 119.7 all-gather.18
  137.4 117.5 all-gather.16
  380.5 46.2 all-gather.26
  428.2 45.6 all-gather.24
  475.4 45.6 all-gather.22
  522.5 45.6 all-gather.28
  569.8 45.6 all-gather.30
  617.1 117.3 all-gather.20
